TPU v7x, 32 devices: a whole 2x2x4 slice. The times are simulated.
32 devices in a mesh: job: 4 (over y, x), zero: 2 (over core), cols: 4 (over z).
Axes of the slice: x: 2, y: 2, z: 4, core: 2. Of those that a mesh axis runs over, the one named last changes fastest.
Arguments:
- weight_gate: bfloat16 [8192, 8192], P(('job', 'zero'), 'cols'), parts along dimension 0, may hold values from -0.1875 to 0.1875
- low_gate: bfloat16 [8192, 32], P(('job', 'zero')), parts along dimension 0, may hold values from -0.125 to 0.125
- high_gate: bfloat16 [128, 8192], P('job', 'cols'), parts along dimension 0, may hold values from -1 to 1
- weight_up: bfloat16 [8192, 8192], P(('job', 'zero'), 'cols'), parts along dimension 0, may hold values from -0.1875 to 0.1875
- low_up: bfloat16 [8192, 32], P(('job', 'zero')), parts along dimension 0, may hold values from -0.125 to 0.125
- high_up: bfloat16 [128, 8192], P('job', 'cols'), parts along dimension 0, may hold values from -1 to 1
- norm_train: float32 [8192], P(('job', 'zero', 'cols')), parts along dimension 0, may hold values from 0.25 to 1.75
- norm_step: float32 [8192], P(('job', 'zero', 'cols')), parts along dimension 0, may hold values from -0.3 to 0.3
Outputs:
- serving_gate: bfloat16 [8192, 8192], P('job', 'cols'), parts along dimension 0
- serving_up: bfloat16 [8192, 8192], P('job', 'cols'), parts along dimension 0
- column_gate: float32 [32768], P(('job', 'cols')), parts along dimension 0
- column_up: float32 [32768], P(('job', 'cols')), parts along dimension 0
- serve_norm: bfloat16 [8192], P('job'), parts along dimension 0
There are 4 independent parts, one for each index of `job`. A program takes and returns all parts, laid end to end along the dimension named above; each array names one. Nothing has to cross between parts.
All inputs are finite; a program needn't handle non-finite values. Where the computation divides by a largest or mean magnitude, that divisor is 1e-20 or more.
Results may differ from a plain program's by a relative error of at most 0.001.
Values may be sent and summed in bfloat16 or wider, within the bound.
A program may use at most 128 MiB of HBM per device.

v0:
```python
import jax
import jax.numpy as jnp
from jax import lax
from jax.sharding import PartitionSpec as P

mix_rate = 2.0


def per_device(weight_gate, low_gate, high_gate, weight_up, low_up, high_up, norm_train, norm_step):
    whole_gate = weight_gate.astype(jnp.float32) + mix_rate * jnp.dot(
        low_gate, high_gate, preferred_element_type=jnp.float32
    )
    whole_up = weight_up.astype(jnp.float32) + mix_rate * jnp.dot(
        low_up, high_up, preferred_element_type=jnp.float32
    )
    column_gate, column_up = lax.pmax(
        (jnp.max(jnp.abs(whole_gate), axis=0), jnp.max(jnp.abs(whole_up), axis=0)), "zero"
    )
    narrow_gate, narrow_up = (
        (whole_gate / column_gate).astype(jnp.bfloat16),
        (whole_up / column_up).astype(jnp.bfloat16),
    )
    serving_gate, serving_up = (
        lax.all_gather(narrow_gate, "zero", axis=0, tiled=True),
        lax.all_gather(narrow_up, "zero", axis=0, tiled=True),
    )
    serve_norm = lax.all_gather(
        (norm_train + norm_step).astype(jnp.bfloat16), ("zero", "cols"), axis=0, tiled=True
    )
    return (serving_gate, serving_up, column_gate, column_up, serve_norm)


def solution(mesh):
    in_specs = (
        P(("job", "zero"), "cols"),
        P(("job", "zero"), None),
        P("job", "cols"),
        P(("job", "zero"), "cols"),
        P(("job", "zero"), None),
        P("job", "cols"),
        P(("job", "zero", "cols")),
        P(("job", "zero", "cols")),
    )
    out_specs = (
        P("job", "cols"),
        P("job", "cols"),
        P(("job", "cols")),
        P(("job", "cols")),
        P("job"),
    )
    return jax.shard_map(
        per_device, mesh=mesh, in_specs=in_specs, out_specs=out_specs, check_vma=False
    )
```

profile of v0, /device:TPU:0, one launch (start us, length us, event | category | flops | bytes accessed | tf_op | source)
XLA Modules:
  0.0 99.6 jit_solution(11368256446369310817)
XLA Ops:
  7.2 0.0 copy-start
  7.2 0.0 copy-start.4
  7.2 0.0 copy-start.3
  7.2 0.0 all-gather.6.cloned.1.call-start
  7.3 0.8 copy-done
  8.1 0.0 copy-start.2
  8.1 7.0 %abs_reduce_fusion.1 = (f32[2048]{0:T(1024)S(1)}, f32[1024,2048]{1,0:T(8,128)}) fusion(bf16[1024,2048]{1,0:T(8,128)(2,1)} %param.8, bf16[1024,32]{0,1:T(8,128)(2,1)} %param.9, bf16[32,2048]{1,0:T(8,128)(2,1)S(1)} %copy-done), kind=kOutput, calls=%fused_computation.4 | convolution fusion | flops 144701440 | bytes 12787712 | tf_op jit(solution)/shard_map/dot_general | solution.py:10
  15.1 0.0 copy-done.4
  15.1 0.0 copy-done.3
  15.1 0.0 copy-done.2
  15.1 4.7 %abs_reduce_fusion = (f32[2048]{0:T(1024)S(1)}, f32[1024,2048]{1,0:T(8,128)}) fusion(bf16[1024,2048]{1,0:T(8,128)(2,1)S(1)} %copy-done.2, bf16[1024,32]{0,1:T(8,128)(2,1)S(1)} %copy-done.4, bf16[32,2048]{1,0:T(8,128)(2,1)S(1)} %copy-done.3), kind=kOutput, calls=%fused_computation.1 | convolution fusion | flops 144701440 | bytes 12787712 | tf_op jit(solution)/shard_map/dot_general | solution.py:13
  19.8 3.6 %all-reduce = (f32[2048]{0:T(1024)S(1)}, f32[2048]{0:T(1024)S(1)}) all-reduce(f32[2048]{0:T(1024)S(1)} %get-tuple-element.7, f32[2048]{0:T(1024)S(1)} %get-tuple-element.9), channel_id=1, replica_groups=mesh['job'=4,'zero'=2,'cols'=4] {'zero'}, use_global_device_ids=true, to_apply=%region_1.0 | all-reduce | flops 4096 | bytes 32768 | tf_op jit(solution)/shard_map/pmax | solution.py:16
  23.4 0.0 copy-start.6
  23.4 0.0 copy-start.5
  23.4 6.8 %divide_convert_fusion = bf16[1024,2048]{1,0:T(8,128)(2,1)} fusion(f32[1024,2048]{1,0:T(8,128)} %get-tuple-element.10, bf16[1024,2048]{1,0:T(8,128)(2,1)} %param.11, f32[2048]{0:T(1024)S(1)} %get-tuple-element.19), kind=kLoop, calls=%fused_computation | loop fusion | flops 10485760 | bytes 16785408 | tf_op jit(solution)/shard_map/convert_element_type | solution.py:21
  30.2 0.0 copy-done.6
  30.2 0.0 all-gather.6.cloned.1.call-update
  30.3 0.0 all-gather.4.cloned.1.call-start
  30.3 0.0 copy-done.5
  30.3 0.0 copy-start.7
  30.3 0.0 copy-start.8
  30.4 6.8 %divide_convert_fusion.1 = bf16[1024,2048]{1,0:T(8,128)(2,1)} fusion(f32[1024,2048]{1,0:T(8,128)} %get-tuple-element.8, bf16[1024,2048]{1,0:T(8,128)(2,1)} %param.8, f32[2048]{0:T(1024)S(1)} %get-tuple-element.18), kind=kLoop, calls=%fused_computation.3 | loop fusion | flops 10485760 | bytes 16785408 | tf_op jit(solution)/shard_map/convert_element_type | solution.py:20
  37.1 0.0 all-gather.4.cloned.1.call-update
  37.2 0.0 copy-done.7
  37.2 0.0 copy-done.8
  37.2 17.5 %all-gather = bf16[8,1,256]{2,1,0:T(2,128)(2,1)S(1)} all-gather(bf16[1,1,256]{2,1,0:T(2,128)(2,1)S(1)} %reshape.12), channel_id=1, replica_groups=mesh['job'=4,'zero'=2,'cols'=4] {'zero','cols'}, dimensions={0}, use_global_device_ids=true | all-gather | bytes 4608 | tf_op jit(solution)/shard_map/all_gather | solution.py:27
  54.7 0.6 copy.13
  55.3 0.0 all-gather.6.cloned.1.call-done
  55.3 20.6 %all-gather.4.cloned.1.call-done = bf16[2048,2048]{1,0:T(8,128)(2,1)} async-done(((bf16[1024,2048]{1,0:T(8,128)(2,1)}), bf16[2048,2048]{1,0:T(8,128)(2,1)}) %all-gather.4.cloned.1.call-update) | async-done | bytes 8388624 | tf_op jit(solution)/shard_map/all_gather | solution.py:24
  75.9 0.0 copy-start.1
  75.9 8.5 %copy.16 = bf16[2048,2048]{1,0:T(8,128)(2,1)} copy(bf16[2048,2048]{1,0:T(8,128)(2,1)} %all-gather.4.cloned.1.call-done) | data formatting | bytes 16777216
  84.3 8.4 %copy.17 = bf16[2048,2048]{1,0:T(8,128)(2,1)} copy(bf16[2048,2048]{1,0:T(8,128)(2,1)} %all-gather.6.cloned.1.call-done) | data formatting | bytes 16777216
  92.8 0.0 copy-done.1
  (3 shorter events, 0.0 us)
Async XLA Ops:
  7.2 0.9 copy-start
  7.2 7.9 %copy-start.4 = (bf16[1024,32]{0,1:T(8,128)(2,1)S(1)}, bf16[1024,32]{0,1:T(8,128)(2,1)}, u32[]{:S(2)}) copy-start(bf16[1024,32]{0,1:T(8,128)(2,1)} %param.12) | copy-start | bytes 196612
  7.2 7.9 %copy-start.3 = (bf16[32,2048]{1,0:T(8,128)(2,1)S(1)}, bf16[32,2048]{1,0:T(8,128)(2,1)}, u32[]{:S(2)}) copy-start(bf16[32,2048]{1,0:T(8,128)(2,1)} %param.13) | copy-start | bytes 393220
  7.2 48.1 %all-gather.6.cloned.1.call-start = ((), (), s32[]{:S(2)}) async-start(), calls=%async_computation.1 | async-start | bytes 12582912 | tf_op jit(solution)/shard_map/all_gather | solution.py:25
  8.1 7.1 %copy-start.2 = (bf16[1024,2048]{1,0:T(8,128)(2,1)S(1)}, bf16[1024,2048]{1,0:T(8,128)(2,1)}, u32[]{:S(2)}) copy-start(bf16[1024,2048]{1,0:T(8,128)(2,1)} %param.11) | copy-start | bytes 12582916
  23.4 6.8 %copy-start.6 = (f32[2048]{0:T(1024)}, f32[2048]{0:T(1024)S(1)}, u32[]{:S(2)}) copy-start(f32[2048]{0:T(1024)S(1)} %get-tuple-element.19) | copy-start | bytes 24580
  23.4 6.9 %copy-start.5 = (f32[2048]{0:T(1024)}, f32[2048]{0:T(1024)S(1)}, u32[]{:S(2)}) copy-start(f32[2048]{0:T(1024)S(1)} %get-tuple-element.18) | copy-start | bytes 24580
  30.3 45.6 %all-gather.4.cloned.1.call-start = ((), (), s32[]{:S(2)}) async-start(), calls=%async_computation | async-start | bytes 12582912 | tf_op jit(solution)/shard_map/all_gather | solution.py:24
  30.3 6.8 %copy-start.7 = (f32[256]{0:T(256)S(1)}, f32[256]{0:T(256)}, u32[]{:S(2)}) copy-start(f32[256]{0:T(256)} %param.14) | copy-start | bytes 3076
  30.3 6.8 %copy-start.8 = (f32[256]{0:T(256)S(1)}, f32[256]{0:T(256)}, u32[]{:S(2)}) copy-start(f32[256]{0:T(256)} %param.15) | copy-start | bytes 3076
  75.9 16.9 %copy-start.1 = (bf16[32,2048]{1,0:T(8,128)(2,1)S(1)}, bf16[32,2048]{1,0:T(8,128)(2,1)}, u32[]{:S(2)}) copy-start(bf16[32,2048]{1,0:T(8,128)(2,1)} %param.10) | copy-start | bytes 393220
Sparse Core Ops, SparseCore 0:
  30.4 22.2 all-gather.5
  54.8 21.0 all-gather.3
where the time goes:
time: 99.8 us; the launch traced here: 99.6 us
  blocking collectives  21.1 us (21%)
  waiting for transfers between devices  20.6 us (21%)
  local copies, waits for them, and re-layouts  18.4 us (18%)
  between operations  14.1 us (14%)
  other arithmetic  13.6 us (14%)
  matrix products  11.7 us (12%)
    all_gather x1, waiting for transfers between devices, per_device(): lax.all_gather(narrow_gate, 'zero', axis=0, tiled=True)  20.6 us
    unnamed x22, local copies, waits for them, and re-layouts  18.4 us
    all_gather x1, blocking collectives, per_device(): lax.all_gather((norm_train + norm_step).astype(jnp.bfloat16), ('zero', 'c...  17.5 us
    dot_general x1, matrix products, per_device(): jnp.dot(low_gate, high_gate, preferred_element_type=jnp.float32)  7.04 us
    convert_element_type x1, other arithmetic, per_device(): (whole_up / column_up).astype(jnp.bfloat16)  6.8 us
    convert_element_type x1, other arithmetic, per_device(): (whole_gate / column_gate).astype(jnp.bfloat16)  6.78 us
    dot_general x1, matrix products, per_device(): jnp.dot(low_up, high_up, preferred_element_type=jnp.float32)  4.69 us
    pmax x1, blocking collectives, per_device(): lax.pmax((jnp.max(jnp.abs(whole_gate), axis=0), jnp.max(jnp.abs(whole_up)...  3.6 us
  transfers between devices with their start and end apart: 2, of which 1 were waited for; matrix products, arithmetic and copies ran while one was open for 7% of the time, Pallas kernels for 0%

commit v1 on v0

v1 whole, which is shorter than its diff:
```python
import functools

import jax
import jax.numpy as jnp
from jax import lax
from jax.experimental import pallas as pl
from jax.experimental.pallas import tpu as pltpu
from jax.sharding import PartitionSpec as P

mix_rate = 2.0
MESH = pl.DeviceIdType.MESH


def small_kernel(zeros, cols, lows, *refs):
    train_ref, step_ref = refs[:2]
    low_refs = refs[2:2 + lows]
    norm_ref = refs[2 + lows]
    got_refs = refs[3 + lows:3 + 2 * lows]
    landed = refs[3 + 2 * lows:3 + 3 * lows]
    mine, slots, norm_send, norm_recv, low_send, low_recv = refs[3 + 3 * lows:]
    group = zeros * cols
    zero, col = lax.axis_index("zero"), lax.axis_index("cols")
    me = zero * cols + col

    def device(rank):
        return {"zero": rank // cols, "cols": lax.rem(rank, cols)}

    barrier = pltpu.get_barrier_semaphore()
    for s in range(1, group):
        pl.semaphore_signal(barrier, inc=1, device_id=device(lax.rem(me + s, group)), device_id_type=MESH)
    mine[...] = train_ref[...] + step_ref[...]
    pl.semaphore_wait(barrier, group - 1)

    copies = []
    for s in range(1, zeros):
        for k in range(lows):
            copies.append(pltpu.make_async_remote_copy(
                src_ref=low_refs[k], dst_ref=landed[k].at[s - 1],
                send_sem=low_send.at[k, s - 1], recv_sem=low_recv.at[k, s - 1],
                device_id={"zero": lax.rem(zero + s, zeros), "cols": col}, device_id_type=MESH))
            copies[-1].start()
    for s in range(1, group):
        copy = pltpu.make_async_remote_copy(
            src_ref=mine, dst_ref=slots.at[me],
            send_sem=norm_send.at[s - 1], recv_sem=norm_recv.at[s - 1],
            device_id=device(lax.rem(me + s, group)), device_id_type=MESH)
        copy.start()
        copies.append(copy)
    for k in range(lows):
        got_refs[k][0] = low_refs[k][...].T
    for copy in copies:
        copy.wait()
    for k in range(lows):
        for s in range(1, zeros):
            got_refs[k][s] = landed[k][s - 1].T
    norm_ref[...] = slots[...].astype(norm_ref.dtype)
    norm_ref[me] = mine[...].astype(norm_ref.dtype)


def exchange_small(zeros, cols, train, step, lows):
    group = zeros * cols
    piece = train.shape[0]
    outs = pl.pallas_call(
        functools.partial(small_kernel, zeros, cols, len(lows)),
        out_shape=[jax.ShapeDtypeStruct((group, 1, piece), jnp.bfloat16)]
        + [jax.ShapeDtypeStruct((zeros,) + low.shape, low.dtype) for low in lows],
        in_specs=[pl.BlockSpec(memory_space=pltpu.VMEM)] * (2 + len(lows)),
        out_specs=[pl.BlockSpec(memory_space=pltpu.VMEM)] * (1 + len(lows)),
        scratch_shapes=[
            pltpu.VMEM((zeros - 1,) + low.shape[::-1], low.dtype) for low in lows
        ] + [
            pltpu.VMEM((1, piece), jnp.float32),
            pltpu.VMEM((group, 1, piece), jnp.float32),
            pltpu.SemaphoreType.DMA((group - 1,)),
            pltpu.SemaphoreType.DMA((group - 1,)),
            pltpu.SemaphoreType.DMA((len(lows), zeros - 1)),
            pltpu.SemaphoreType.DMA((len(lows), zeros - 1)),
        ],
        cost_estimate=pl.CostEstimate(flops=0, bytes_accessed=2 ** 22, transcendentals=0),
        compiler_params=pltpu.CompilerParams(collective_id=0, has_side_effects=True),
    )(train.reshape(1, piece), step.reshape(1, piece), *[low.T for low in lows])
    return outs[0].reshape(group * piece), outs[1:]


def merge_kernel(zeros, chunk, *refs):
    weight_refs = refs[:zeros]
    low_ref, high_ref, out_ref, column_ref, whole = refs[zeros:]
    zero = lax.axis_index("zero")
    rows, width = weight_refs[0].shape
    high = high_ref[...] * jnp.bfloat16(mix_rate)
    most = jnp.zeros((8, width), jnp.float32)
    for s in range(zeros):
        def step(i, most, s=s):
            at = pl.ds(pl.multiple_of(i * chunk, chunk), chunk)
            low = low_ref[s, at, :]
            value = weight_refs[s][at, :].astype(jnp.float32) + jnp.dot(
                low, high, preferred_element_type=jnp.float32)
            whole[s, at, :] = value
            return jnp.maximum(most, jnp.max(jnp.abs(value).reshape(chunk // 8, 8, width), axis=0))
        most = lax.fori_loop(0, rows // chunk, step, most, unroll=True)
    column = jnp.max(most, axis=0, keepdims=True)
    column_ref[...] = column
    scale = 1.0 / column
    for s in range(zeros):
        base = lax.rem(zero - s + zeros, zeros) * rows

        def put(i, carry, s=s, base=base):
            start = pl.multiple_of(i * chunk, chunk)
            out_ref[pl.ds(pl.multiple_of(base + start, chunk), chunk), :] = (
                whole[s, pl.ds(start, chunk), :] * scale).astype(out_ref.dtype)
            return carry
        lax.fori_loop(0, rows // chunk, put, 0, unroll=True)


def merge(zeros, weights, low, high):
    rows, columns = weights[0].shape
    rank = low.shape[2]
    width = min(256, columns)
    chunk = min(128, rows)
    serving, column = pl.pallas_call(
        functools.partial(merge_kernel, zeros, chunk),
        grid=(columns // width,),
        out_shape=[
            jax.ShapeDtypeStruct((rows * zeros, columns), jnp.bfloat16),
            jax.ShapeDtypeStruct((1, columns), jnp.float32),
        ],
        in_specs=[pl.BlockSpec((rows, width), lambda j: (0, j))] * zeros + [
            pl.BlockSpec((zeros, rows, rank), lambda j: (0, 0, 0)),
            pl.BlockSpec((rank, width), lambda j: (0, j)),
        ],
        out_specs=[
            pl.BlockSpec((rows * zeros, width), lambda j: (0, j)),
            pl.BlockSpec((1, width), lambda j: (0, j)),
        ],
        scratch_shapes=[pltpu.VMEM((zeros, rows, width), jnp.float32)],
        cost_estimate=pl.CostEstimate(
            flops=2 * rows * zeros * columns * rank,
            bytes_accessed=4 * rows * zeros * columns, transcendentals=0),
        compiler_params=pltpu.CompilerParams(dimension_semantics=("arbitrary",)),
    )(*weights, low, high)
    return serving, column.reshape(columns)


def per_device(zeros, cols, weight_gate, low_gate, high_gate, weight_up, low_up, high_up, norm_train, norm_step):
    def moved(array):
        return [array] + [
            lax.ppermute(array, "zero", [(i, (i + s) % zeros) for i in range(zeros)])
            for s in range(1, zeros)
        ]

    gates, ups = moved(weight_gate), moved(weight_up)
    serve_norm, (all_gate, all_up) = exchange_small(
        zeros, cols, norm_train, norm_step, (low_gate, low_up))
    serving_gate, column_gate = merge(zeros, gates, all_gate, high_gate)
    serving_up, column_up = merge(zeros, ups, all_up, high_up)
    return (serving_gate, serving_up, column_gate, column_up, serve_norm)


def solution(mesh):
    in_specs = (
        P(("job", "zero"), "cols"),
        P(("job", "zero"), None),
        P("job", "cols"),
        P(("job", "zero"), "cols"),
        P(("job", "zero"), None),
        P("job", "cols"),
        P(("job", "zero", "cols")),
        P(("job", "zero", "cols")),
    )
    out_specs = (
        P("job", "cols"),
        P("job", "cols"),
        P(("job", "cols")),
        P(("job", "cols")),
        P("job"),
    )
    return jax.shard_map(
        functools.partial(per_device, mesh.shape["zero"], mesh.shape["cols"]),
        mesh=mesh, in_specs=in_specs, out_specs=out_specs, check_vma=False
    )
```

time: 99.8 us -> 39.9 us (0.40)
  the two profiles are of different devices: /device:TPU:0 before, /device:TPU:7 now
where the time goes in v1:
time: 39.9 us; the launch traced here: 39.3 us
  Pallas kernels  36.5 us (91%)
  starting transfers between devices  0.82 us (2%)
  other arithmetic  0.73 us (2%)
  between operations  0.65 us (2%)
  local copies, waits for them, and re-layouts  0.6 us (2%)
    pallas_call x2, Pallas kernels, merge(): pl.pallas_call(functools.partial(merge_kernel, zeros, chunk), grid=(colum...  22 us
    pallas_call x1, Pallas kernels, exchange_small(): pl.pallas_call(functools.partial(small_kernel, zeros, cols, len(lows)), o...  14.5 us
    ppermute x2, starting transfers between devices, moved(): lax.ppermute(array, 'zero', [(i, (i + s) % zeros) for i in range(zeros)])  0.82 us
  transfers between devices with their start and end apart: 2, of which 0 were waited for; matrix products, arithmetic and copies ran while one was open for 3% of the time, Pallas kernels for 65%

profile of v1, /device:TPU:7, one launch (start us, length us, event | category | flops | bytes accessed | tf_op | source)
XLA Modules:
  0.0 39.3 jit_solution(1455115424578339163)
XLA Ops:
  0.6 0.7 %collective-permute-start = (bf16[1024,2048]{1,0:T(8,128)(2,1)}, bf16[1024,2048]{1,0:T(8,128)(2,1)}, u32[]{:S(2)}, u32[]{:S(2)}) collective-permute-start(bf16[1024,2048]{1,0:T(8,128)(2,1)} %refs_0_.2), channel_id=1, source_target_pairs={{0,4},{4,0},{1,5},{5,1},{2,6},{6,2},{3,7},{7,3},{8,12},{12,8},{9,1... | collective-permute-start | bytes 12582920 | tf_op jit(solution)/shard_map/ppermute | solution.py:147
  1.4 0.1 collective-permute-start.1
  1.5 14.5 %shard_map.119 = (bf16[8,1,256]{2,1,0:T(2,128)(2,1)}, bf16[2,1024,32]{2,1,0:T(8,128)(2,1)}, bf16[2,1024,32]{2,1,0:T(8,128)(2,1)}) custom-call(f32[1,256]{1,0:T(1,128)} %bitcast.12, f32[1,256]{1,0:T(1,128)} %bitcast.13, bf16[32,1024]{1,0:T(8,128)(2,1)} %bitcast.8, bf16[32,1024]{1,0:T(8,128)(2,1)} %bitcast.9), custom_call_target="tpu_custom_call" | custom-call | bytes 4194304 | tf_op jit(solution)/shard_map/pallas_call | solution.py:63
  15.9 0.7 %reduce = bf16[8,256]{1,0:T(8,128)(2,1)S(1)} reduce(bf16[8,1,256]{2,1,0:T(2,128)(2,1)} %get-tuple-element.18, bf16[]{:T(256)} %constant), dimensions={1}, to_apply=%get-tuple-element.18.reduce_sub_computation | reduce | bytes 8194 | tf_op jit(solution)/shard_map/pallas_call | solution.py:63
  16.7 0.6 %copy.13 = bf16[1,2,8,128]{3,1,2,0:T(2,128)(2,1)} copy(bf16[1,2,8,128]{3,2,1,0:T(8,128)(2,1)S(1)} %bitcast.10) | data formatting | bytes 8192
  17.3 0.0 collective-permute-done.refs_1_
  17.3 11.0 %shard_map.120 = (bf16[2048,2048]{1,0:T(8,128)(2,1)}, f32[1,2048]{1,0:T(1,128)}) custom-call(bf16[1024,2048]{1,0:T(8,128)(2,1)} %refs_0_.2, bf16[1024,2048]{1,0:T(8,128)(2,1)} %collective-permute-done.refs_1_, bf16[2,1024,32]{2,1,0:T(8,128)(2,1)} %get-tuple-element.12.refs_2_, bf16[32,2048]{1,0:T(8,128)(2,1)} %refs_3_.2), custom_call_target="tpu_custom_call" | custom-call | flops 268435456 | bytes 16777216 | tf_op jit(solution)/shard_map/pallas_call | solution.py:120
  28.3 0.0 collective-permute-done.1.refs_1_
  28.3 11.0 %shard_map.121 = (bf16[2048,2048]{1,0:T(8,128)(2,1)}, f32[1,2048]{1,0:T(1,128)}) custom-call(bf16[1024,2048]{1,0:T(8,128)(2,1)} %refs_0_.3, bf16[1024,2048]{1,0:T(8,128)(2,1)} %collective-permute-done.1.refs_1_, bf16[2,1024,32]{2,1,0:T(8,128)(2,1)} %get-tuple-element.14.refs_2_, bf16[32,2048]{1,0:T(8,128)(2,1)} %refs_3_.3), custom_call_target="tpu_custom_call" | custom-call | flops 268435456 | bytes 16777216 | tf_op jit(solution)/shard_map/pallas_call | solution.py:120
Async XLA Ops:
  0.6 16.6 %collective-permute-start = (bf16[1024,2048]{1,0:T(8,128)(2,1)}, bf16[1024,2048]{1,0:T(8,128)(2,1)}, u32[]{:S(2)}, u32[]{:S(2)}) collective-permute-start(bf16[1024,2048]{1,0:T(8,128)(2,1)} %refs_0_.2), channel_id=1, source_target_pairs={{0,4},{4,0},{1,5},{5,1},{2,6},{6,2},{3,7},{7,3},{8,12},{12,8},{9,1... | collective-permute-start | bytes 12582920 | tf_op jit(solution)/shard_map/ppermute | solution.py:147
  1.4 26.9 %collective-permute-start.1 = (bf16[1024,2048]{1,0:T(8,128)(2,1)}, bf16[1024,2048]{1,0:T(8,128)(2,1)}, u32[]{:S(2)}, u32[]{:S(2)}) collective-permute-start(bf16[1024,2048]{1,0:T(8,128)(2,1)} %refs_0_.3), channel_id=1, source_target_pairs={{0,4},{4,0},{1,5},{5,1},{2,6},{6,2},{3,7},{7,3},{8,12},{12,8},{9,1... | collective-permute-start | bytes 12582920 | tf_op jit(solution)/shard_map/ppermute | solution.py:147

commit v2 on v1

--- a/solution.py
+++ b/solution.py
@@ -11,13 +11,15 @@
 MESH = pl.DeviceIdType.MESH
 
 
-def small_kernel(zeros, cols, lows, *refs):
+def first_kernel(zeros, cols, lows, weight_ref, *refs):
     train_ref, step_ref = refs[:2]
     low_refs = refs[2:2 + lows]
     norm_ref = refs[2 + lows]
     got_refs = refs[3 + lows:3 + 2 * lows]
-    landed = refs[3 + 2 * lows:3 + 3 * lows]
-    mine, slots, norm_send, norm_recv, low_send, low_recv = refs[3 + 3 * lows:]
+    moved_refs = refs[3 + 2 * lows:2 + 2 * lows + zeros]
+    refs = refs[2 + 2 * lows + zeros:]
+    landed = refs[:lows]
+    mine, slots, norm_send, norm_recv, low_send, low_recv, weight_send, weight_recv = refs[lows:]
     group = zeros * cols
     zero, col = lax.axis_index("zero"), lax.axis_index("cols")
     me = zero * cols + col
@@ -39,6 +41,11 @@
                 send_sem=low_send.at[k, s - 1], recv_sem=low_recv.at[k, s - 1],
                 device_id={"zero": lax.rem(zero + s, zeros), "cols": col}, device_id_type=MESH))
             copies[-1].start()
+    for s in range(1, zeros):
+        copies.append(pltpu.make_async_remote_copy(
+            src_ref=weight_ref, dst_ref=moved_refs[s - 1],
+            send_sem=weight_send.at[s - 1], recv_sem=weight_recv.at[s - 1],
+            device_id={"zero": lax.rem(zero + s, zeros), "cols": col}, device_id_type=MESH))
     for s in range(1, group):
         copy = pltpu.make_async_remote_copy(
             src_ref=mine, dst_ref=slots.at[me],
@@ -46,6 +53,8 @@
             device_id=device(lax.rem(me + s, group)), device_id_type=MESH)
         copy.start()
         copies.append(copy)
+    for copy in copies[lows * (zeros - 1):(1 + lows) * (zeros - 1)]:
+        copy.start()
     for k in range(lows):
         got_refs[k][0] = low_refs[k][...].T
     for copy in copies:
@@ -53,33 +62,38 @@
     for k in range(lows):
         for s in range(1, zeros):
             got_refs[k][s] = landed[k][s - 1].T
-    norm_ref[...] = slots[...].astype(norm_ref.dtype)
-    norm_ref[me] = mine[...].astype(norm_ref.dtype)
+    slots[me] = mine[...]
+    norm_ref[...] = jnp.concatenate([slots[g] for g in range(group)], axis=0).astype(norm_ref.dtype)
 
 
-def exchange_small(zeros, cols, train, step, lows):
+def exchange_first(zeros, cols, weight, train, step, lows):
     group = zeros * cols
-    piece = train.shape[0]
+    lanes = 128 if train.shape[0] % 128 == 0 else train.shape[0]
+    tall = train.shape[0] // lanes
     outs = pl.pallas_call(
-        functools.partial(small_kernel, zeros, cols, len(lows)),
-        out_shape=[jax.ShapeDtypeStruct((group, 1, piece), jnp.bfloat16)]
-        + [jax.ShapeDtypeStruct((zeros,) + low.shape, low.dtype) for low in lows],
-        in_specs=[pl.BlockSpec(memory_space=pltpu.VMEM)] * (2 + len(lows)),
-        out_specs=[pl.BlockSpec(memory_space=pltpu.VMEM)] * (1 + len(lows)),
+        functools.partial(first_kernel, zeros, cols, len(lows)),
+        out_shape=[jax.ShapeDtypeStruct((group * tall, lanes), jnp.bfloat16)]
+        + [jax.ShapeDtypeStruct((zeros,) + low.shape, low.dtype) for low in lows]
+        + [jax.ShapeDtypeStruct(weight.shape, weight.dtype)] * (zeros - 1),
+        in_specs=[pl.BlockSpec(memory_space=pl.ANY)] + [pl.BlockSpec(memory_space=pltpu.VMEM)] * (2 + len(lows)),
+        out_specs=[pl.BlockSpec(memory_space=pltpu.VMEM)] * (1 + len(lows))
+        + [pl.BlockSpec(memory_space=pl.ANY)] * (zeros - 1),
         scratch_shapes=[
             pltpu.VMEM((zeros - 1,) + low.shape[::-1], low.dtype) for low in lows
         ] + [
-            pltpu.VMEM((1, piece), jnp.float32),
-            pltpu.VMEM((group, 1, piece), jnp.float32),
+            pltpu.VMEM((tall, lanes), jnp.float32),
+            pltpu.VMEM((group, tall, lanes), jnp.float32),
             pltpu.SemaphoreType.DMA((group - 1,)),
             pltpu.SemaphoreType.DMA((group - 1,)),
             pltpu.SemaphoreType.DMA((len(lows), zeros - 1)),
             pltpu.SemaphoreType.DMA((len(lows), zeros - 1)),
+            pltpu.SemaphoreType.DMA((zeros - 1,)),
+            pltpu.SemaphoreType.DMA((zeros - 1,)),
         ],
         cost_estimate=pl.CostEstimate(flops=0, bytes_accessed=2 ** 22, transcendentals=0),
         compiler_params=pltpu.CompilerParams(collective_id=0, has_side_effects=True),
-    )(train.reshape(1, piece), step.reshape(1, piece), *[low.T for low in lows])
-    return outs[0].reshape(group * piece), outs[1:]
+    )(weight, train.reshape(tall, lanes), step.reshape(tall, lanes), *[low.T for low in lows])
+    return outs[0].reshape(group * tall * lanes), outs[1:1 + len(lows)], outs[1 + len(lows):]
 
 
 def merge_kernel(zeros, chunk, *refs):
@@ -115,7 +129,7 @@
 def merge(zeros, weights, low, high):
     rows, columns = weights[0].shape
     rank = low.shape[2]
-    width = min(256, columns)
+    width = min(512, columns)
     chunk = min(128, rows)
     serving, column = pl.pallas_call(
         functools.partial(merge_kernel, zeros, chunk),
@@ -136,7 +150,7 @@
         cost_estimate=pl.CostEstimate(
             flops=2 * rows * zeros * columns * rank,
             bytes_accessed=4 * rows * zeros * columns, transcendentals=0),
-        compiler_params=pltpu.CompilerParams(dimension_semantics=("arbitrary",)),
+        compiler_params=pltpu.CompilerParams(dimension_semantics=("arbitrary",), vmem_limit_bytes=60 * 2 ** 20),
     )(*weights, low, high)
     return serving, column.reshape(columns)
 
@@ -148,10 +162,11 @@
             for s in range(1, zeros)
         ]
 
-    gates, ups = moved(weight_gate), moved(weight_up)
-    serve_norm, (all_gate, all_up) = exchange_small(
-        zeros, cols, norm_train, norm_step, (low_gate, low_up))
-    serving_gate, column_gate = merge(zeros, gates, all_gate, high_gate)
+    serve_norm, (all_gate, all_up), gates = exchange_first(
+        zeros, cols, weight_gate, norm_train, norm_step, (low_gate, low_up))
+    weight_up, all_up = lax.optimization_barrier((weight_up, all_up))
+    ups = moved(weight_up)
+    serving_gate, column_gate = merge(zeros, [weight_gate, *gates], all_gate, high_gate)
     serving_up, column_up = merge(zeros, ups, all_up, high_up)
     return (serving_gate, serving_up, column_gate, column_up, serve_norm)
 

time: 39.9 us -> 36 us (0.902)
  the two profiles are of different devices: /device:TPU:7 before, /device:TPU:0 now
where the time goes in v2:
time: 36 us; the launch traced here: 35.8 us
  Pallas kernels  34.1 us (95%)
  between operations  0.65 us (2%)
  local copies, waits for them, and re-layouts  0.6 us (2%)
  starting transfers between devices  0.44 us (1%)
    pallas_call x2, Pallas kernels, merge(): pl.pallas_call(functools.partial(merge_kernel, zeros, chunk), grid=(colum...  19.6 us
    pallas_call x1, Pallas kernels, exchange_first(): pl.pallas_call(functools.partial(first_kernel, zeros, cols, len(lows)), o...  14.5 us
  transfers between devices with their start and end apart: 1, of which 0 were waited for; matrix products, arithmetic and copies ran while one was open for 0% of the time, Pallas kernels for 27%

profile of v2, /device:TPU:0, one launch (start us, length us, event | category | flops | bytes accessed | tf_op | source)
XLA Modules:
  0.0 35.8 jit_solution(18384597503846192527)
XLA Ops:
  0.6 14.5 %shard_map.119 = (bf16[16,128]{1,0:T(8,128)(2,1)}, bf16[2,1024,32]{2,1,0:T(8,128)(2,1)}, bf16[2,1024,32]{2,1,0:T(8,128)(2,1)}, bf16[1024,2048]{1,0:T(8,128)(2,1)}) custom-call(bf16[1024,2048]{1,0:T(8,128)(2,1)} %refs_0_.1, f32[2,128]{1,0:T(2,128)} %bitcast.10, f32[2,128]{1,0:T(2,128)} %bitcast.11, bf16[32,1024]{1,0:T(8,128)(2,1)} %bitcast.7, ...), custom_call_target="tpu_custom_call" | custom-call | bytes 4194304 | tf_op jit(solution)/shard_map/pallas_call | solution.py:73
  15.2 0.4 %collective-permute-start = (bf16[1024,2048]{1,0:T(8,128)(2,1)}, bf16[1024,2048]{1,0:T(8,128)(2,1)}, u32[]{:S(2)}, u32[]{:S(2)}) collective-permute-start(bf16[1024,2048]{1,0:T(8,128)(2,1)} %refs_0_.2), channel_id=1, source_target_pairs={{0,4},{4,0},{1,5},{5,1},{2,6},{6,2},{3,7},{7,3},{8,12},{12,8},{9,1... | collective-permute-start | bytes 12582920 | tf_op jit(solution)/shard_map/ppermute | solution.py:161
  15.6 9.8 %shard_map.120 = (bf16[2048,2048]{1,0:T(8,128)(2,1)}, f32[1,2048]{1,0:T(1,128)}) custom-call(bf16[1024,2048]{1,0:T(8,128)(2,1)} %refs_0_.1, bf16[1024,2048]{1,0:T(8,128)(2,1)} %get-tuple-element.15.refs_1_, bf16[2,1024,32]{2,1,0:T(8,128)(2,1)} %get-tuple-element.16.refs_2_, bf16[32,2048]{1,0:T(8,128)(2,1)} %refs_3_.2), custom_call_target="tpu_custom_call" | custom-call | flops 268435456 | bytes 16777216 | tf_op jit(solution)/shard_map/pallas_call | solution.py:134
  25.4 0.0 copy-start
  25.4 0.0 collective-permute-done.refs_1_
  25.4 9.8 %shard_map.121 = (bf16[2048,2048]{1,0:T(8,128)(2,1)}, f32[1,2048]{1,0:T(1,128)}) custom-call(bf16[1024,2048]{1,0:T(8,128)(2,1)} %refs_0_.2, bf16[1024,2048]{1,0:T(8,128)(2,1)} %collective-permute-done.refs_1_, bf16[2,1024,32]{2,1,0:T(8,128)(2,1)} %get-tuple-element.20.refs_2_, bf16[32,2048]{1,0:T(8,128)(2,1)} %refs_3_.3), custom_call_target="tpu_custom_call" | custom-call | flops 268435456 | bytes 16777216 | tf_op jit(solution)/shard_map/pallas_call | solution.py:134
  35.2 0.0 copy-done
  35.2 0.6 %copy.14 = bf16[2048]{0:T(1024)(128)(2,1)} copy(bf16[2048]{0:T(1024)(128)(2,1)S(1)} %bitcast.9) | data formatting | bytes 8192
Async XLA Ops:
  15.2 10.2 %collective-permute-start = (bf16[1024,2048]{1,0:T(8,128)(2,1)}, bf16[1024,2048]{1,0:T(8,128)(2,1)}, u32[]{:S(2)}, u32[]{:S(2)}) collective-permute-start(bf16[1024,2048]{1,0:T(8,128)(2,1)} %refs_0_.2), channel_id=1, source_target_pairs={{0,4},{4,0},{1,5},{5,1},{2,6},{6,2},{3,7},{7,3},{8,12},{12,8},{9,1... | collective-permute-start | bytes 12582920 | tf_op jit(solution)/shard_map/ppermute | solution.py:161
  25.4 9.8 %copy-start = (bf16[16,128]{1,0:T(8,128)(2,1)S(1)}, bf16[16,128]{1,0:T(8,128)(2,1)}, u32[]{:S(2)}) copy-start(bf16[16,128]{1,0:T(8,128)(2,1)} %get-tuple-element.24) | copy-start | bytes 12292

commit v3 on v1

--- a/solution.py
+++ b/solution.py
@@ -53,24 +53,25 @@
     for k in range(lows):
         for s in range(1, zeros):
             got_refs[k][s] = landed[k][s - 1].T
-    norm_ref[...] = slots[...].astype(norm_ref.dtype)
-    norm_ref[me] = mine[...].astype(norm_ref.dtype)
+    slots[me] = mine[...]
+    norm_ref[...] = jnp.concatenate([slots[g] for g in range(group)], axis=0).astype(norm_ref.dtype)
 
 
 def exchange_small(zeros, cols, train, step, lows):
     group = zeros * cols
-    piece = train.shape[0]
+    lanes = 128 if train.shape[0] % 128 == 0 else train.shape[0]
+    tall = train.shape[0] // lanes
     outs = pl.pallas_call(
         functools.partial(small_kernel, zeros, cols, len(lows)),
-        out_shape=[jax.ShapeDtypeStruct((group, 1, piece), jnp.bfloat16)]
+        out_shape=[jax.ShapeDtypeStruct((group * tall, lanes), jnp.bfloat16)]
         + [jax.ShapeDtypeStruct((zeros,) + low.shape, low.dtype) for low in lows],
         in_specs=[pl.BlockSpec(memory_space=pltpu.VMEM)] * (2 + len(lows)),
         out_specs=[pl.BlockSpec(memory_space=pltpu.VMEM)] * (1 + len(lows)),
         scratch_shapes=[
             pltpu.VMEM((zeros - 1,) + low.shape[::-1], low.dtype) for low in lows
         ] + [
-            pltpu.VMEM((1, piece), jnp.float32),
-            pltpu.VMEM((group, 1, piece), jnp.float32),
+            pltpu.VMEM((tall, lanes), jnp.float32),
+            pltpu.VMEM((group, tall, lanes), jnp.float32),
             pltpu.SemaphoreType.DMA((group - 1,)),
             pltpu.SemaphoreType.DMA((group - 1,)),
             pltpu.SemaphoreType.DMA((len(lows), zeros - 1)),
@@ -78,8 +79,8 @@
         ],
         cost_estimate=pl.CostEstimate(flops=0, bytes_accessed=2 ** 22, transcendentals=0),
         compiler_params=pltpu.CompilerParams(collective_id=0, has_side_effects=True),
-    )(train.reshape(1, piece), step.reshape(1, piece), *[low.T for low in lows])
-    return outs[0].reshape(group * piece), outs[1:]
+    )(train.reshape(tall, lanes), step.reshape(tall, lanes), *[low.T for low in lows])
+    return outs[0].reshape(group * tall * lanes), outs[1:]
 
 
 def merge_kernel(zeros, chunk, *refs):
@@ -115,7 +116,7 @@
 def merge(zeros, weights, low, high):
     rows, columns = weights[0].shape
     rank = low.shape[2]
-    width = min(256, columns)
+    width = min(512, columns)
     chunk = min(128, rows)
     serving, column = pl.pallas_call(
         functools.partial(merge_kernel, zeros, chunk),
@@ -136,7 +137,7 @@
         cost_estimate=pl.CostEstimate(
             flops=2 * rows * zeros * columns * rank,
             bytes_accessed=4 * rows * zeros * columns, transcendentals=0),
-        compiler_params=pltpu.CompilerParams(dimension_semantics=("arbitrary",)),
+        compiler_params=pltpu.CompilerParams(dimension_semantics=("arbitrary",), vmem_limit_bytes=60 * 2 ** 20),
     )(*weights, low, high)
     return serving, column.reshape(columns)
 

time: 39.9 us -> 36.4 us (0.912)
  the two profiles are of different devices: /device:TPU:7 before, /device:TPU:0 now
where the time goes in v3:
time: 36.4 us; the launch traced here: 35.9 us
  Pallas kernels  34 us (93%)
  between operations  0.66 us (2%)
  starting transfers between devices  0.64 us (2%)
  local copies, waits for them, and re-layouts  0.6 us (2%)
    pallas_call x2, Pallas kernels, merge(): pl.pallas_call(functools.partial(merge_kernel, zeros, chunk), grid=(colum...  19.5 us
    pallas_call x1, Pallas kernels, exchange_small(): pl.pallas_call(functools.partial(small_kernel, zeros, cols, len(lows)), o...  14.5 us
  transfers between devices with their start and end apart: 2, of which 0 were waited for; matrix products, arithmetic and copies ran while one was open for 0% of the time, Pallas kernels for 67%

profile of v3, /device:TPU:0, one launch (start us, length us, event | category | flops | bytes accessed | tf_op | source)
XLA Modules:
  0.0 35.9 jit_solution(5972077256587993594)
XLA Ops:
  0.6 0.6 %collective-permute-start = (bf16[1024,2048]{1,0:T(8,128)(2,1)}, bf16[1024,2048]{1,0:T(8,128)(2,1)}, u32[]{:S(2)}, u32[]{:S(2)}) collective-permute-start(bf16[1024,2048]{1,0:T(8,128)(2,1)} %refs_0_.2), channel_id=1, source_target_pairs={{0,4},{4,0},{1,5},{5,1},{2,6},{6,2},{3,7},{7,3},{8,12},{12,8},{9,1... | collective-permute-start | bytes 12582920 | tf_op jit(solution)/shard_map/ppermute | solution.py:148
  1.2 0.1 collective-permute-start.1
  1.3 14.5 %shard_map.119 = (bf16[16,128]{1,0:T(8,128)(2,1)}, bf16[2,1024,32]{2,1,0:T(8,128)(2,1)}, bf16[2,1024,32]{2,1,0:T(8,128)(2,1)}) custom-call(f32[2,128]{1,0:T(2,128)} %bitcast.10, f32[2,128]{1,0:T(2,128)} %bitcast.11, bf16[32,1024]{1,0:T(8,128)(2,1)} %bitcast.7, bf16[32,1024]{1,0:T(8,128)(2,1)} %bitcast.8), custom_call_target="tpu_custom_call" | custom-call | bytes 4194304 | tf_op jit(solution)/shard_map/pallas_call | solution.py:64
  15.7 0.0 collective-permute-done.refs_1_
  15.7 9.8 %shard_map.120 = (bf16[2048,2048]{1,0:T(8,128)(2,1)}, f32[1,2048]{1,0:T(1,128)}) custom-call(bf16[1024,2048]{1,0:T(8,128)(2,1)} %refs_0_.2, bf16[1024,2048]{1,0:T(8,128)(2,1)} %collective-permute-done.refs_1_, bf16[2,1024,32]{2,1,0:T(8,128)(2,1)} %get-tuple-element.12.refs_2_, bf16[32,2048]{1,0:T(8,128)(2,1)} %refs_3_.2), custom_call_target="tpu_custom_call" | custom-call | flops 268435456 | bytes 16777216 | tf_op jit(solution)/shard_map/pallas_call | solution.py:121
  25.5 0.0 collective-permute-done.1.refs_1_
  25.5 0.0 copy-start
  25.5 9.8 %shard_map.121 = (bf16[2048,2048]{1,0:T(8,128)(2,1)}, f32[1,2048]{1,0:T(1,128)}) custom-call(bf16[1024,2048]{1,0:T(8,128)(2,1)} %refs_0_.3, bf16[1024,2048]{1,0:T(8,128)(2,1)} %collective-permute-done.1.refs_1_, bf16[2,1024,32]{2,1,0:T(8,128)(2,1)} %get-tuple-element.14.refs_2_, bf16[32,2048]{1,0:T(8,128)(2,1)} %refs_3_.3), custom_call_target="tpu_custom_call" | custom-call | flops 268435456 | bytes 16777216 | tf_op jit(solution)/shard_map/pallas_call | solution.py:121
  35.3 0.0 copy-done
  35.3 0.6 %copy.14 = bf16[2048]{0:T(1024)(128)(2,1)} copy(bf16[2048]{0:T(1024)(128)(2,1)S(1)} %bitcast.9) | data formatting | bytes 8192
Async XLA Ops:
  0.6 15.1 %collective-permute-start = (bf16[1024,2048]{1,0:T(8,128)(2,1)}, bf16[1024,2048]{1,0:T(8,128)(2,1)}, u32[]{:S(2)}, u32[]{:S(2)}) collective-permute-start(bf16[1024,2048]{1,0:T(8,128)(2,1)} %refs_0_.2), channel_id=1, source_target_pairs={{0,4},{4,0},{1,5},{5,1},{2,6},{6,2},{3,7},{7,3},{8,12},{12,8},{9,1... | collective-permute-start | bytes 12582920 | tf_op jit(solution)/shard_map/ppermute | solution.py:148
  1.2 24.3 %collective-permute-start.1 = (bf16[1024,2048]{1,0:T(8,128)(2,1)}, bf16[1024,2048]{1,0:T(8,128)(2,1)}, u32[]{:S(2)}, u32[]{:S(2)}) collective-permute-start(bf16[1024,2048]{1,0:T(8,128)(2,1)} %refs_0_.3), channel_id=1, source_target_pairs={{0,4},{4,0},{1,5},{5,1},{2,6},{6,2},{3,7},{7,3},{8,12},{12,8},{9,1... | collective-permute-start | bytes 12582920 | tf_op jit(solution)/shard_map/ppermute | solution.py:148
  25.5 9.8 %copy-start = (bf16[16,128]{1,0:T(8,128)(2,1)S(1)}, bf16[16,128]{1,0:T(8,128)(2,1)}, u32[]{:S(2)}) copy-start(bf16[16,128]{1,0:T(8,128)(2,1)} %get-tuple-element.18) | copy-start | bytes 12292
